TPU v7x, 8 devices: a whole 2x2x1 slice. The times are simulated.
8 devices in a mesh: dp: 8 (over z, y, x, core).
Axes of the slice: x: 2, y: 2, z: 1, core: 2. Of those that a mesh axis runs over, the one named last changes fastest.
Arguments:
- x_saved: bfloat16 [16, 768, 2048], P('dp')
- grad_out: bfloat16 [16, 768, 2048], P('dp')
- positions: int32 [16, 768], P('dp')
- attn_gain: bfloat16 [2048], replicated
- w_query: bfloat16 [2048, 16, 128], replicated
- w_key: bfloat16 [2048, 16, 128], replicated
- w_value: bfloat16 [2048, 16, 128], replicated
- w_out: bfloat16 [16, 128, 2048], replicated
- mlp_gain: bfloat16 [2048], replicated
- w_gate: bfloat16 [2048, 5504], replicated
- w_up: bfloat16 [2048, 5504], replicated
- w_down: bfloat16 [5504, 2048], replicated
- master_flat: float32 [50597888], P('dp')
- adam_mean: float32 [50597888], P('dp')
- adam_var: float32 [50597888], P('dp')
Outputs:
- output 1: bfloat16 [16, 768, 2048], P('dp')
- output 2: bfloat16 [2048], replicated
- output 3: bfloat16 [2048, 16, 128], replicated
- output 4: bfloat16 [2048, 16, 128], replicated
- output 5: bfloat16 [2048, 16, 128], replicated
- output 6: bfloat16 [16, 128, 2048], replicated
- output 7: bfloat16 [2048], replicated
- output 8: bfloat16 [2048, 5504], replicated
- output 9: bfloat16 [2048, 5504], replicated
- output 10: bfloat16 [5504, 2048], replicated
- output 11: float32 [50597888], P('dp')
- output 12: float32 [50597888], P('dp')
- output 13: float32 [50597888], P('dp')
- output 14: float32 [], replicated
All inputs are finite; a program needn't handle non-finite values.
Results may differ from a plain program's by a relative error of at most 0.0125245.
Values are sent between devices in bfloat16 or wider.
A program may use at most 1.5 GiB of HBM per device.

v0:
```python
import jax
import jax.numpy as jnp
from jax import lax
from jax.sharding import PartitionSpec as P

NORM_EPS = 1e-5
ROPE_BASE = 10000.0
LEARN_RATE = 2e-3
BETA_ONE = 0.9
BETA_TWO = 0.95
ADAM_EPS = 1e-8
WEIGHT_DECAY = 0.1
STEP_COUNT = 100


def rope_tables(positions, head_dim):
    half_dim = head_dim // 2
    inv_freq = ROPE_BASE ** (-2.0 * jnp.arange(half_dim, dtype=jnp.float32) / head_dim)
    angles = positions.astype(jnp.float32)[:, :, None] * inv_freq
    cos_full = jnp.concatenate([jnp.cos(angles), jnp.cos(angles)], axis=-1)[:, :, None, :]
    sin_full = jnp.concatenate([jnp.sin(angles), jnp.sin(angles)], axis=-1)[:, :, None, :]
    return cos_full, sin_full


def rope_apply(values, cos_full, sin_full):
    half_dim = values.shape[-1] // 2
    rotated = jnp.concatenate([-values[..., half_dim:], values[..., :half_dim]], axis=-1)
    return values * cos_full + rotated * sin_full


def rope_back(grad_rot, cos_full, sin_full):
    half_dim = grad_rot.shape[-1] // 2
    scaled = grad_rot * sin_full
    return grad_rot * cos_full + jnp.concatenate([scaled[..., half_dim:], -scaled[..., :half_dim]], axis=-1)


def rms_parts(values):
    inv_rms = lax.rsqrt(jnp.mean(values * values, axis=-1, keepdims=True) + NORM_EPS)
    return inv_rms, values * inv_rms


def rms_back(d_normed, gain_wide, inv_rms, x_hat):
    d_hat = d_normed * gain_wide
    return inv_rms * (d_hat - x_hat * jnp.mean(d_hat * x_hat, axis=-1, keepdims=True))


def local_grads(x_loc, dy_loc, pos_loc, w_list):
    attn_gain, w_query, w_key, w_value, w_out, mlp_gain, w_gate, w_up, w_down = w_list
    num_seqs, seq_len, model_dim = x_loc.shape
    num_heads, head_dim = w_query.shape[1], w_query.shape[2]
    kv_heads = w_key.shape[1]
    group_size = num_heads // kv_heads
    n_tok = num_seqs * seq_len
    wq_flat = w_query.reshape(model_dim, num_heads * head_dim)
    wk_flat = w_key.reshape(model_dim, kv_heads * head_dim)
    wv_flat = w_value.reshape(model_dim, kv_heads * head_dim)
    wo_flat = w_out.reshape(num_heads * head_dim, model_dim)
    dy_flat = dy_loc.reshape(n_tok, model_dim)
    x_wide = x_loc.reshape(n_tok, model_dim).astype(jnp.float32)
    inv_one, value_a8 = rms_parts(x_wide)
    gain_one = attn_gain.astype(jnp.float32)
    normed = (value_a8 * gain_one).astype(jnp.bfloat16)
    q_pre = jnp.dot(normed, wq_flat, preferred_element_type=jnp.float32).reshape(num_seqs, seq_len, num_heads, head_dim)
    k_pre = jnp.dot(normed, wk_flat, preferred_element_type=jnp.float32).reshape(num_seqs, seq_len, kv_heads, head_dim)
    v_heads = jnp.dot(normed, wv_flat, preferred_element_type=jnp.float32).astype(jnp.bfloat16).reshape(num_seqs, seq_len, kv_heads, head_dim)
    cos_full, sin_full = rope_tables(pos_loc, head_dim)
    q_rot = rope_apply(q_pre, cos_full, sin_full).astype(jnp.bfloat16).reshape(num_seqs, seq_len, kv_heads, group_size, head_dim)
    k_rot = rope_apply(k_pre, cos_full, sin_full).astype(jnp.bfloat16)
    score_scale = head_dim ** -0.5
    scores = jnp.einsum('bqkgd,bskd->bkgqs', q_rot, k_rot, preferred_element_type=jnp.float32) * score_scale
    causal = lax.iota(jnp.int32, seq_len)[:, None] >= lax.iota(jnp.int32, seq_len)[None, :]
    attn_probs = jax.nn.softmax(jnp.where(causal, scores, -1e30), axis=-1)
    probs_low = attn_probs.astype(jnp.bfloat16)
    context = jnp.einsum('bkgqs,bskd->bqkgd', probs_low, v_heads, preferred_element_type=jnp.float32).astype(jnp.bfloat16)
    context = context.reshape(n_tok, num_heads * head_dim)
    attn_out = jnp.dot(context, wo_flat, preferred_element_type=jnp.float32)
    hidden = (x_wide + attn_out).astype(jnp.bfloat16)
    inv_two, array_b8 = rms_parts(hidden.astype(jnp.float32))
    gain_two = mlp_gain.astype(jnp.float32)
    normed_mlp = (array_b8 * gain_two).astype(jnp.bfloat16)
    gate_pre = jnp.dot(normed_mlp, w_gate, preferred_element_type=jnp.float32)
    up_pre = jnp.dot(normed_mlp, w_up, preferred_element_type=jnp.float32)
    gate_sig = jax.nn.sigmoid(gate_pre)
    gate_act = gate_pre * gate_sig
    gated_act = (gate_act * up_pre).astype(jnp.bfloat16)
    g_down = jnp.einsum('nf,nd->fd', gated_act, dy_flat, preferred_element_type=jnp.float32)
    d_gated = jnp.einsum('nd,fd->nf', dy_flat, w_down, preferred_element_type=jnp.float32)
    d_up = (d_gated * gate_act).astype(jnp.bfloat16)
    d_gate = (d_gated * up_pre * gate_sig * (1.0 + gate_pre * (1.0 - gate_sig))).astype(jnp.bfloat16)
    g_gate = jnp.einsum('nd,nf->df', normed_mlp, d_gate, preferred_element_type=jnp.float32)
    g_up = jnp.einsum('nd,nf->df', normed_mlp, d_up, preferred_element_type=jnp.float32)
    d_normed_mlp = (jnp.einsum('nf,df->nd', d_gate, w_gate, preferred_element_type=jnp.float32)
                    + jnp.einsum('nf,df->nd', d_up, w_up, preferred_element_type=jnp.float32))
    g_mlp_gain = jnp.sum(d_normed_mlp * array_b8, axis=0)
    d_hidden = rms_back(d_normed_mlp, gain_two, inv_two, array_b8) + dy_flat.astype(jnp.float32)
    d_hidden_low = d_hidden.astype(jnp.bfloat16)
    g_out = jnp.einsum('nc,nd->cd', context, d_hidden_low, preferred_element_type=jnp.float32)
    d_context = jnp.einsum('nd,cd->nc', d_hidden_low, wo_flat, preferred_element_type=jnp.float32).astype(jnp.bfloat16)
    d_context = d_context.reshape(num_seqs, seq_len, kv_heads, group_size, head_dim)
    d_probs = jnp.einsum('bqkgd,bskd->bkgqs', d_context, v_heads, preferred_element_type=jnp.float32)
    g_values = jnp.einsum('bkgqs,bqkgd->bskd', probs_low, d_context, preferred_element_type=jnp.float32)
    d_scores = (attn_probs * (d_probs - jnp.sum(d_probs * attn_probs, axis=-1, keepdims=True)) * score_scale).astype(jnp.bfloat16)
    d_q_rot = jnp.einsum('bkgqs,bskd->bqkgd', d_scores, k_rot, preferred_element_type=jnp.float32).reshape(num_seqs, seq_len, num_heads, head_dim)
    d_k_rot = jnp.einsum('bkgqs,bqkgd->bskd', d_scores, q_rot, preferred_element_type=jnp.float32)
    d_q_pre = rope_back(d_q_rot, cos_full, sin_full).astype(jnp.bfloat16).reshape(n_tok, num_heads * head_dim)
    d_k_pre = rope_back(d_k_rot, cos_full, sin_full).astype(jnp.bfloat16).reshape(n_tok, kv_heads * head_dim)
    d_v_pre = g_values.astype(jnp.bfloat16).reshape(n_tok, kv_heads * head_dim)
    g_query = jnp.einsum('nd,nc->dc', normed, d_q_pre, preferred_element_type=jnp.float32)
    g_key = jnp.einsum('nd,nc->dc', normed, d_k_pre, preferred_element_type=jnp.float32)
    g_value = jnp.einsum('nd,nc->dc', normed, d_v_pre, preferred_element_type=jnp.float32)
    d_normed = (jnp.einsum('nc,dc->nd', d_q_pre, wq_flat, preferred_element_type=jnp.float32)
                + jnp.einsum('nc,dc->nd', d_k_pre, wk_flat, preferred_element_type=jnp.float32)
                + jnp.einsum('nc,dc->nd', d_v_pre, wv_flat, preferred_element_type=jnp.float32))
    g_attn_gain = jnp.sum(d_normed * value_a8, axis=0)
    d_x = rms_back(d_normed, gain_one, inv_one, value_a8) + d_hidden
    grad_list = [g_attn_gain, g_query, g_key, g_value, g_out, g_mlp_gain, g_gate, g_up, g_down]
    flat_grad = jnp.concatenate([w_grad.astype(jnp.bfloat16).reshape(-1) for w_grad in grad_list])
    return d_x.astype(jnp.bfloat16).reshape(num_seqs, seq_len, model_dim), flat_grad


def gain_offset(w_list):
    return w_list[0].shape[0] + w_list[1].size + w_list[2].size + w_list[3].size + w_list[4].size


def adamw_apply(grad_vec, grad_norm, master_vec, mean_vec, var_vec, first_index, model_dim, gain_two):
    clip_scale = jnp.minimum(1.0, 1.0 / (grad_norm + 1e-6))
    clipped = grad_vec * clip_scale
    new_mean = BETA_ONE * mean_vec + (1.0 - BETA_ONE) * clipped
    new_var = BETA_TWO * var_vec + (1.0 - BETA_TWO) * clipped * clipped
    mean_hat = new_mean / (1.0 - BETA_ONE ** STEP_COUNT)
    var_hat = new_var / (1.0 - BETA_TWO ** STEP_COUNT)
    flat_index = first_index + lax.iota(jnp.int32, master_vec.shape[0])
    is_gain = (flat_index < model_dim) | ((flat_index >= gain_two) & (flat_index < gain_two + model_dim))
    decays = jnp.where(is_gain, 0.0, WEIGHT_DECAY)
    new_master = master_vec - LEARN_RATE * (mean_hat / (jnp.sqrt(var_hat) + ADAM_EPS) + decays * master_vec)
    return new_master, new_mean, new_var


def split_flat(flat_vec, w_list):
    pieces = []
    offset = 0
    for weight in w_list:
        pieces.append(flat_vec[offset:offset + weight.size].reshape(weight.shape))
        offset += weight.size
    return pieces


def solution(mesh):
    dp_size = mesh.shape['dp']

    def per_device(x_loc, dy_loc, pos_loc, attn_gain, w_query, w_key, w_value, w_out, mlp_gain, w_gate, w_up, w_down, master_loc, mean_loc, var_loc):
        w_list = (attn_gain, w_query, w_key, w_value, w_out, mlp_gain, w_gate, w_up, w_down)
        grad_x, flat_grad = local_grads(x_loc, dy_loc, pos_loc, w_list)
        grad_shard = lax.psum_scatter(flat_grad, 'dp', scatter_dimension=0, tiled=True).astype(jnp.float32) / dp_size
        grad_norm = jnp.sqrt(lax.psum(jnp.sum(grad_shard * grad_shard), 'dp'))
        shard_len = master_loc.shape[0]
        shard_start = lax.axis_index('dp') * shard_len
        new_master, new_mean, new_var = adamw_apply(grad_shard, grad_norm, master_loc, mean_loc, var_loc, shard_start, attn_gain.shape[0], gain_offset(w_list))
        gathered = lax.all_gather(new_master.astype(jnp.bfloat16), 'dp', tiled=True)
        new_weights = split_flat(gathered, w_list)
        return (grad_x,) + tuple(new_weights) + (new_master, new_mean, new_var, grad_norm)

    in_specs = (P('dp'),) * 3 + (P(),) * 9 + (P('dp'),) * 3
    out_specs = (P('dp'),) + (P(),) * 9 + (P('dp'),) * 3 + (P(),)
    return jax.shard_map(per_device, mesh=mesh, in_specs=in_specs, out_specs=out_specs, check_vma=False)
```

profile of v0, /device:TPU:0, one launch (start us, length us, event | category | flops | bytes accessed | tf_op | source)
XLA Modules:
  0.0 4799.1 jit_solution(4959100820619668954)
XLA Ops:
  147.4 23.3 fusion.38
  170.7 31.3 fusion.6
  202.0 24.1 fusion.5
  226.1 32.5 convert_bitcast_fusion.5
  288.8 45.7 fusion.112
  334.4 46.2 fusion.114
  380.6 48.5 %fusion.54 = bf16[688,16,8,128]{3,2,1,0:T(8,128)(2,1)} fusion(bf16[1536,2048]{1,0:T(8,128)(2,1)} %bitcast.252, f32[1536,5504]{1,0:T(8,128)} %fusion.114, f32[1536,5504]{1,0:T(8,128)} %fusion.112), kind=kOutput, calls=%fused_computation.85 | convolution fusion | flops 34690170880 | bytes 96468992 | tf_op jit(solution)/shard_map/nf,nd->fd/dot_general | solution.py:86
  429.1 64.4 %multiply_convert_fusion.1 = (bf16[1536,5504]{1,0:T(8,128)(2,1)}, bf16[1536,5504]{1,0:T(8,128)(2,1)}) fusion(f32[1536,5504]{1,0:T(8,128)} %fusion.112, f32[1536,5504]{1,0:T(8,128)} %fusion.114, bf16[1536,2048]{1,0:T(8,128)(2,1)} %bitcast.253, bf16[5504,2048]{1,0:T(8,128)(2,1)} %param.26), kind=kOutput, calls=%fused_computation.18 | convolution fusion | flops 34738077696 | bytes 130285568 | tf_op jit(solution)/shard_map/nd,fd->nf/dot_general | solution.py:87
  493.5 46.3 fusion.124
  539.8 48.1 %convolution_convert_fusion.2 = bf16[2048,5504]{1,0:T(8,128)(2,1)} fusion(bf16[1536,5504]{1,0:T(8,128)(2,1)} %get-tuple-element.43, bf16[1536,2048]{1,0:T(8,128)(2,1)S(1)} %copy-done.6, f32[2048]{0:T(1024)S(1)} %copy-done.21, f32[1536]{0:T(1024)S(1)} %copy-done.23), kind=kOutput, calls=%fused_computation.39 | convolution fusion | flops 34652028928 | bytes 45758464 | tf_op jit(solution)/shard_map/nd,nf->df/dot_general | solution.py:90
  587.9 48.2 %convolution_convert_fusion.1 = bf16[2048,5504]{1,0:T(8,128)(2,1)} fusion(bf16[1536,5504]{1,0:T(8,128)(2,1)} %get-tuple-element.42, bf16[1536,2048]{1,0:T(8,128)(2,1)S(1)} %copy-done.6, f32[2048]{0:T(1024)S(1)} %copy-done.21, f32[1536]{0:T(1024)S(1)} %copy-done.23), kind=kOutput, calls=%fused_computation.38 | convolution fusion | flops 34652028928 | bytes 45758464 | tf_op jit(solution)/shard_map/nd,nf->df/dot_general | solution.py:91
  636.1 51.2 %fusion.33 = (bf16[2048]{0:T(1024)(128)(2,1)}, f32[1536]{0:T(1024)S(1)}, f32[1536,2048]{1,0:T(8,128)}) fusion(bf16[1536,2048]{1,0:T(8,128)(2,1)} %get-tuple-element.63, f32[1536]{0:T(1024)S(1)} %copy-done.23, f32[2048]{0:T(1024)S(1)} %copy-done.21, f32[1536,2048]{1,0:T(8,128)} %fusion.124, bf16[1536,5504]{1,0:T(8,128)(2,1)} %get-tuple-element.42, ...), kind=kOutput, calls=%fused_computation.51 | convolution fusion | flops 34653339648 | bytes 70934528 | tf_op jit(solution)/shard_map/nf,df->nd/dot_general | solution.py:93
  754.2 33.3 convert_bitcast_fusion.4
  787.5 56.1 %fusion = (f32[2,16,768]{2,1,0:T(8,128)S(1)}, f32[2,16,768,768]{3,2,1,0:T(8,128)}) fusion(f32[2,16,768]{2,1,0:T(8,128)S(1)} %copy-done.14, f32[2,16,768]{2,1,0:T(8,128)S(1)} %copy-done.12, f32[2,16,768,768]{3,2,1,0:T(8,128)} %get-tuple-element.61, pred[768,768]{0,1:T(8,128)(4,1)S(1)} %copy-done.1, bf16[2,768,16,128]{1,3,2,0:T(8,128)(2,1)} %copy.70, ...), kind=kOutput, calls=%fused_computation.3 | convolution fusion | flops 4945059840 | bytes 164462592 | tf_op jit(solution)/shard_map/bqkgd,bskd->bkgqs/dot_general | solution.py:100
  843.5 60.7 %fusion.7 = bf16[2,16,768,768]{2,3,1,0:T(8,128)(2,1)} fusion(f32[2,16,768,768]{3,2,1,0:T(8,128)} %get-tuple-element.66, f32[2,16,768]{2,1,0:T(8,128)S(1)} %get-tuple-element.65, f32[2,16,768]{2,1,0:T(8,128)S(1)} %copy-done.14, f32[2,16,768]{2,1,0:T(8,128)S(1)} %copy-done.12, f32[2,16,768,768]{3,2,1,0:T(8,128)} %get-tuple-element.61, ...), kind=kLoop, calls=%fused_computation.12 | loop fusion | flops 150994944 | bytes 189628416 | tf_op jit(solution)/shard_map/reshape.9
  925.9 31.2 bitcast_multiply_fusion.1
  979.0 23.1 fusion.40
  1112.9 43.4 reshape.327
  1156.4 43.4 reshape.328
  1258.1 27.0 fusion.49
  1356.7 1116.0 %all-reduce.3.cloned.1.call-done = bf16[50597888]{0:T(1024)(128)(2,1)} async-done(((bf16[50597888]{0:T(1024)(128)(2,1)}), bf16[50597888]{0:T(1024)(128)(2,1)}) %all-reduce.3.cloned.1.call-update) | async-done | bytes 101195792
  2507.1 67.0 %fusion.116 = (bf16[6324736]{0:T(1024)(128)(2,1)}, f32[6324736]{0:T(1024)}, f32[6324736]{0:T(1024)}, f32[6324736]{0:T(1024)}) fusion(f32[6324736]{0:T(1024)} %param.27, s32[]{:T(128)S(6)} %mul.342, f32[]{:T(128)S(6)} %mul.332, bf16[50597888]{0:T(1024)(128)(2,1)} %all-reduce.3.cloned.1.call-done, u32[]{:T(128)S(6)} %multiply.39, f32[6324736]{0:T(1024)} %param.28, ...), kind=kLoop, calls=%fused_computation.161 | loop fusion | flops 158118400 | bytes 177092624 | tf_op jit(solution)/shard_map/convert_element_type | solution.py:159
  2574.1 150.5 %while = (u32[]{:T(128)}, bf16[6324736]{0:T(1024)(128)(2,1)}, bf16[1,1,6324736]{2,1,0:T(2,128)(2,1)}) while((u32[]{:T(128)}, bf16[6324736]{0:T(1024)(128)(2,1)}, bf16[1,1,6324736]{2,1,0:T(2,128)(2,1)}) %tuple.43), condition=%cond, body=%body | while | flops 9 | bytes 50598028
  2579.5 145.1 %reshape_dynamic-update-slice_fusion = bf16[1,1,6324736]{2,1,0:T(2,128)(2,1)} fusion(bf16[1,1,6324736]{2,1,0:T(2,128)(2,1)} %get-tuple-element.81, u32[]{:T(128)S(6)} %multiply.40, u32[]{:T(128)S(6)} %multiply.41, bf16[6324736]{0:T(1024)(128)(2,1)S(1)} %dynamic-slice.4), kind=kLoop, calls=%fused_computation.167 | loop fusion | bytes 25298952
  2739.2 858.4 %all-gather.3.cloned.1.call-done = bf16[8,1,6324736]{2,1,0:T(2,128)(2,1)} async-done(((bf16[1,1,6324736]{2,1,0:T(2,128)(2,1)}), bf16[8,1,6324736]{2,1,0:T(2,128)(2,1)}) %all-gather.3.cloned.1.call-update) | async-done | bytes 101195792 | tf_op jit(solution)/shard_map/all_gather | solution.py:159
  3597.6 547.5 %reduce.4 = bf16[8,6324736]{1,0:T(8,128)(2,1)} reduce(bf16[8,1,6324736]{2,1,0:T(2,128)(2,1)} %all-gather.3.cloned.1.call-done, bf16[]{:T(256)} %constant.69), dimensions={1}, to_apply=%all-gather.reduce_sub_computation | reduce | bytes 202391552 | tf_op jit(solution)/shard_map/all_gather | solution.py:159
  4145.2 447.1 %reshape.335 = bf16[50597888]{0:T(1024)(128)(2,1)} reshape(bf16[8,6324736]{1,0:T(8,128)(2,1)} %reduce.4) | data formatting | bytes 202391552
  4593.5 22.7 fusion.121
  4616.2 44.8 fusion.119
  4661.1 33.6 slice.111
  4707.9 41.5 reshape.332
  4749.4 41.5 reshape.331
  (146 shorter events, 589.5 us)
Async XLA Ops:
  7.2 2465.5 %all-reduce.3.cloned.1.call-start = ((), (), s32[]{:S(2)}) async-start(), calls=%async_computation.1 | async-start | bytes 202391552
  7.4 218.7 %copy-start = (pred[768,768]{0,1:T(8,128)(4,1)}, pred[768,768]{0,1:T(8,128)(4,1)S(1)}, u32[]{:S(2)}) copy-start(pred[768,768]{0,1:T(8,128)(4,1)S(1)} %iota_compare_fusion) | copy-start | bytes 1769476
  14.2 23.4 copy-start.15
  19.1 18.5 copy-start.10
  129.2 18.3 copy-start.2
  129.2 18.2 copy-start.4
  202.0 24.1 copy-start.11
  226.1 32.6 copy-start.13
  267.7 21.0 copy-start.20
  288.8 45.7 copy-start.22
  493.5 46.3 copy-start.6
  493.5 46.3 copy-start.21
  493.5 46.3 copy-start.23
  687.3 14.7 copy-start.7
  740.2 14.0 copy-start.1
  740.2 14.0 copy-start.12
  740.3 13.9 copy-start.14
  904.2 21.6 copy-start.3
  968.0 11.0 copy-start.5
  1011.0 19.7 copy-start.8
  1057.0 19.8 copy-start.9
  1057.0 37.4 slice-start.6
  1057.0 37.4 slice-start.7
  1057.0 37.4 slice-start.8
  1057.0 37.4 slice-start.9
  1076.8 17.6 slice-start.10
  1076.8 17.6 slice-start.11
  1248.1 10.0 copy-start.16
  1248.1 10.0 copy-start.18
  1285.1 8.8 slice-start.4
  1285.7 8.2 slice-start.5
  1356.6 2241.0 %all-gather.3.cloned.1.call-start = ((), (), s32[]{:S(2)}) async-start(), calls=%async_computation | async-start | bytes 227690496 | tf_op jit(solution)/shard_map/all_gather | solution.py:159
  (8 other events, 29.9 us)
Sparse Core Ops, SparseCore 0:
  1356.8 1115.9 all-reduce.2
  2724.8 872.7 all-gather.2
where the time goes:
time: 4810 us; the launch traced here: 4800 us
  waiting for transfers between devices  1970 us (41%)
  local copies, waits for them, and re-layouts  1110 us (23%)
  matrix products  841 us (17%)
  other arithmetic  838 us (17%)
    unnamed x3, waiting for transfers between devices  1120 us
    all_gather x1, waiting for transfers between devices, per_device(): gathered = lax.all_gather(new_master.astype(jnp.bfloat16), 'dp', tiled=True)  858 us
    unnamed x96, local copies, waits for them, and re-layouts  735 us
    all_gather x1, other arithmetic, per_device(): gathered = lax.all_gather(new_master.astype(jnp.bfloat16), 'dp', tiled=True)  548 us
    slice x4, local copies, waits for them, and re-layouts, split_flat(): pieces.append(flat_vec[offset:offset + weight.size].reshape(weight.shape))  102 us
    reshape x3, local copies, waits for them, and re-layouts, split_flat(): pieces.append(flat_vec[offset:offset + weight.size].reshape(weight.shape))  96.2 us
  transfers between devices with their start and end apart: 2, of which 2 were waited for; matrix products, arithmetic and copies ran while one was open for 0% of the time, Pallas kernels for 0%

commit v1 on v0

--- a/solution.py
+++ b/solution.py
@@ -1,6 +1,11 @@
+import functools
+
 import jax
 import jax.numpy as jnp
+import numpy as np
 from jax import lax
+from jax.experimental import pallas as pl
+from jax.experimental.pallas import tpu as pltpu
 from jax.sharding import PartitionSpec as P
 
 NORM_EPS = 1e-5
@@ -114,51 +119,378 @@
     g_attn_gain = jnp.sum(d_normed * value_a8, axis=0)
     d_x = rms_back(d_normed, gain_one, inv_one, value_a8) + d_hidden
     grad_list = [g_attn_gain, g_query, g_key, g_value, g_out, g_mlp_gain, g_gate, g_up, g_down]
-    flat_grad = jnp.concatenate([w_grad.astype(jnp.bfloat16).reshape(-1) for w_grad in grad_list])
-    return d_x.astype(jnp.bfloat16).reshape(num_seqs, seq_len, model_dim), flat_grad
-
-
-def gain_offset(w_list):
-    return w_list[0].shape[0] + w_list[1].size + w_list[2].size + w_list[3].size + w_list[4].size
-
-
-def adamw_apply(grad_vec, grad_norm, master_vec, mean_vec, var_vec, first_index, model_dim, gain_two):
-    clip_scale = jnp.minimum(1.0, 1.0 / (grad_norm + 1e-6))
-    clipped = grad_vec * clip_scale
-    new_mean = BETA_ONE * mean_vec + (1.0 - BETA_ONE) * clipped
-    new_var = BETA_TWO * var_vec + (1.0 - BETA_TWO) * clipped * clipped
-    mean_hat = new_mean / (1.0 - BETA_ONE ** STEP_COUNT)
-    var_hat = new_var / (1.0 - BETA_TWO ** STEP_COUNT)
-    flat_index = first_index + lax.iota(jnp.int32, master_vec.shape[0])
-    is_gain = (flat_index < model_dim) | ((flat_index >= gain_two) & (flat_index < gain_two + model_dim))
-    decays = jnp.where(is_gain, 0.0, WEIGHT_DECAY)
-    new_master = master_vec - LEARN_RATE * (mean_hat / (jnp.sqrt(var_hat) + ADAM_EPS) + decays * master_vec)
-    return new_master, new_mean, new_var
-
-
-def split_flat(flat_vec, w_list):
-    pieces = []
-    offset = 0
-    for weight in w_list:
-        pieces.append(flat_vec[offset:offset + weight.size].reshape(weight.shape))
-        offset += weight.size
-    return pieces
+    return d_x.astype(jnp.bfloat16).reshape(num_seqs, seq_len, model_dim), grad_list
+
+
+LANES = 128
+SLAB_ROWS = 49412
+CHUNK_ROWS = 12384
+NUM_CHUNKS = 4
+STEP_ROWS = 4128
+SUB_ROWS = 32
+GRAD_ROWS = NUM_CHUNKS * CHUNK_ROWS + 16
+CARRY_ROWS = 704
+ROW_BASE = {'wq': 16, 'wk': 32784, 'wv': 65552, 'wo': 98320, 'wg': 131104, 'wu': 219168, 'wd': 307232}
+ROW_COUNT = {'wq': 32768, 'wk': 32768, 'wv': 32768, 'wo': 32768, 'wg': 88064, 'wu': 88064, 'wd': 88064}
+GROUP_ROWS = {'wq': 256, 'wk': 256, 'wv': 256, 'wo': 256, 'wg': 688, 'wu': 688, 'wd': 256}
+NAMES = ('wq', 'wk', 'wv', 'wo', 'wg', 'wu', 'wd')
+GAIN_TWO_ROW = 131088
+
+
+def frame_start(owner):
+    return SLAB_ROWS * owner // 16 * 16
+
+
+def frame_stop(owner):
+    return -(-SLAB_ROWS * (owner + 1) // 16) * 16
+
+
+def pieces_of(src):
+    found = []
+    for number, name in enumerate(NAMES):
+        rows = ROW_COUNT[name] // 8
+        start = ROW_BASE[name] + src * rows
+        for owner in range(8):
+            low, high = max(start, frame_start(owner)), min(start + rows, frame_stop(owner))
+            if low < high:
+                found.append((number, owner, low - start, low - frame_start(owner), high - low))
+    return found
+
+
+def regroup_kernel(*refs):
+    shard_refs = refs[:7]
+    gain_ref, sumsq_ref = refs[7:9]
+    grad_ref, gains_out, sums_out = refs[9:12]
+    bounce, gains_in, sums_in, send_sem, recv_sem, small_send, small_recv, local_sem = refs[12:]
+    me = lax.axis_index('dp')
+
+    def piece_copy(number, owner, src, src_row, dst_row, rows, slot):
+        return pltpu.make_async_remote_copy(
+            src_ref=shard_refs[number].at[pl.ds(src_row, rows), :],
+            dst_ref=grad_ref.at[pl.ds(dst_row, rows), :],
+            send_sem=send_sem.at[slot], recv_sem=recv_sem.at[number, src],
+            device_id=(owner,), device_id_type=pl.DeviceIdType.MESH)
+
+    def small_copy(src_ref, dst_ref, number, shift):
+        return pltpu.make_async_remote_copy(
+            src_ref=src_ref, dst_ref=dst_ref.at[me],
+            send_sem=small_send.at[number, shift], recv_sem=small_recv.at[number, shift],
+            device_id=(lax.rem(me + shift, 8),), device_id_type=pl.DeviceIdType.MESH)
+
+    for shift in range(1, 8):
+        small_copy(gain_ref, gains_in, 0, shift).start()
+        small_copy(sumsq_ref, sums_in, 1, shift).start()
+    all_pieces = [pieces_of(src) for src in range(8)]
+    for src in range(8):
+        @pl.when(me == src)
+        def _():
+            for slot, (number, owner, src_row, dst_row, rows) in enumerate(all_pieces[src]):
+                if owner != src:
+                    piece_copy(number, owner, src, src_row, dst_row, rows, slot).start()
+            for number, owner, src_row, dst_row, rows in all_pieces[src]:
+                if owner == src:
+                    part = bounce.at[pl.ds(0, rows), :]
+                    copy_in = pltpu.make_async_copy(shard_refs[number].at[pl.ds(src_row, rows), :], part, local_sem)
+                    copy_in.start()
+                    copy_in.wait()
+                    copy_out = pltpu.make_async_copy(part, grad_ref.at[pl.ds(dst_row, rows), :], local_sem)
+                    copy_out.start()
+                    copy_out.wait()
+    gains_in[me] = gain_ref[...]
+    sums_in[me] = sumsq_ref[...]
+    for shift in range(1, 8):
+        small_copy(gain_ref, gains_in, 0, shift).wait()
+        small_copy(sumsq_ref, sums_in, 1, shift).wait()
+    gains_out[...] = gains_in[...]
+    sums_out[...] = sums_in[...]
+    for dev in range(8):
+        @pl.when(me == dev)
+        def _():
+            for slot, (number, owner, src_row, dst_row, rows) in enumerate(all_pieces[dev]):
+                if owner != dev:
+                    piece_copy(number, owner, dev, src_row, dst_row, rows, slot).wait_send()
+            for src in range(8):
+                for number, owner, src_row, dst_row, rows in all_pieces[src]:
+                    if owner == dev and src != dev:
+                        piece_copy(number, owner, src, src_row, dst_row, rows, 0).wait_recv()
+
+
+def regroup(shards, gain_rows, sumsq):
+    any_spec = pl.BlockSpec(memory_space=pl.ANY)
+    vmem_spec = pl.BlockSpec(memory_space=pltpu.VMEM)
+    return pl.pallas_call(
+        regroup_kernel,
+        out_shape=(jax.ShapeDtypeStruct((GRAD_ROWS, LANES), jnp.bfloat16),
+                   jax.ShapeDtypeStruct((8, 32, LANES), jnp.bfloat16),
+                   jax.ShapeDtypeStruct((8, 8, LANES), jnp.float32)),
+        in_specs=[any_spec] * 7 + [vmem_spec] * 2,
+        out_specs=(any_spec, vmem_spec, vmem_spec),
+        scratch_shapes=[
+            pltpu.VMEM((11008, LANES), jnp.bfloat16),
+            pltpu.VMEM((8, 32, LANES), jnp.bfloat16),
+            pltpu.VMEM((8, 8, LANES), jnp.float32),
+            pltpu.SemaphoreType.DMA((16,)),
+            pltpu.SemaphoreType.DMA((7, 8)),
+            pltpu.SemaphoreType.DMA((2, 8)),
+            pltpu.SemaphoreType.DMA((2, 8)),
+            pltpu.SemaphoreType.DMA,
+        ],
+        compiler_params=pltpu.CompilerParams(has_side_effects=True),
+        name='regroup',
+    )(*shards, gain_rows, sumsq)
+
+
+def adamw_kernel(chunk, me_ref, scale_ref, grad_ref, tail_ref, master_ref, mean_ref, var_ref, *rest):
+    new_master, new_mean, new_var, low_ref, wide = rest[-5:]
+    me = me_ref[0]
+    scale = scale_ref[0]
+    shift = lax.rem(4 * me, 16)
+    wide[pl.ds(0, STEP_ROWS), :] = grad_ref[...].astype(jnp.float32)
+    wide[pl.ds(STEP_ROWS, 16), :] = tail_ref[...].astype(jnp.float32)
+    first_row = me * SLAB_ROWS + (chunk * (CHUNK_ROWS // STEP_ROWS) + pl.program_id(0)) * STEP_ROWS
+
+    def body(number, carry):
+        base = pl.multiple_of(number * SUB_ROWS, SUB_ROWS)
+        rows = pl.ds(base, SUB_ROWS)
+        clipped = wide[pl.ds(base + shift, SUB_ROWS), :] * scale
+        mean = BETA_ONE * mean_ref[rows, :] + (1.0 - BETA_ONE) * clipped
+        var = BETA_TWO * var_ref[rows, :] + (1.0 - BETA_TWO) * clipped * clipped
+        new_mean[rows, :] = mean
+        new_var[rows, :] = var
+        mean_hat = mean / (1.0 - BETA_ONE ** STEP_COUNT)
+        var_hat = var / (1.0 - BETA_TWO ** STEP_COUNT)
+        row = first_row + base + lax.broadcasted_iota(jnp.int32, (SUB_ROWS, LANES), 0)
+        is_gain = (row < 16) | ((row >= GAIN_TWO_ROW) & (row < GAIN_TWO_ROW + 16))
+        decays = jnp.where(is_gain, 0.0, WEIGHT_DECAY)
+        master = master_ref[rows, :]
+        master = master - LEARN_RATE * (mean_hat / (jnp.sqrt(var_hat) + ADAM_EPS) + decays * master)
+        new_master[rows, :] = master
+        low_ref[rows, :] = master.astype(jnp.bfloat16)
+        return carry
+
+    lax.fori_loop(0, STEP_ROWS // SUB_ROWS, body, 0)
+
+
+def adamw_chunk(chunk, me_vec, scale_vec, grad_rows, state, done):
+    steps = CHUNK_ROWS // STEP_ROWS
+    first = chunk * steps
+    block = pl.BlockSpec((STEP_ROWS, LANES), lambda t, *_: (first + t, 0))
+    tail = pl.BlockSpec((16, LANES), lambda t, *_: ((first + t + 1) * (STEP_ROWS // 16), 0))
+    any_spec = pl.BlockSpec(memory_space=pl.ANY)
+    full = jax.ShapeDtypeStruct((SLAB_ROWS, LANES), jnp.float32)
+    return pl.pallas_call(
+        functools.partial(adamw_kernel, chunk),
+        grid_spec=pltpu.PrefetchScalarGridSpec(
+            num_scalar_prefetch=2, grid=(steps,),
+            in_specs=[block, tail, block, block, block] + [any_spec] * len(done),
+            out_specs=(block, block, block, pl.BlockSpec((STEP_ROWS, LANES), lambda t, *_: (t, 0))),
+            scratch_shapes=[pltpu.VMEM((STEP_ROWS + 16, LANES), jnp.float32)]),
+        out_shape=(full, full, full, jax.ShapeDtypeStruct((CHUNK_ROWS, LANES), jnp.bfloat16)),
+        input_output_aliases={7 + n: n for n in range(len(done))},
+        compiler_params=pltpu.CompilerParams(
+            dimension_semantics=('arbitrary',), vmem_limit_bytes=48 * 2 ** 20),
+        cost_estimate=pl.CostEstimate(flops=30 * CHUNK_ROWS * LANES, bytes_accessed=28 * CHUNK_ROWS * LANES,
+                                      transcendentals=0),
+        name=f'adamw_{chunk}',
+    )(me_vec, scale_vec, grad_rows, grad_rows, *state, *done)
+
+
+def group_table(chunk):
+    table = np.zeros((8, 7, 2), np.int32)
+    for slab in range(8):
+        start = SLAB_ROWS * slab
+        for number, name in enumerate(NAMES):
+            size = GROUP_ROWS[name]
+            mine = []
+            for group in range(ROW_COUNT[name] // size):
+                first = ROW_BASE[name] + group * size - start
+                stop = first + size
+                if not 0 <= first < SLAB_ROWS:
+                    continue
+                at = NUM_CHUNKS - 1 if stop > SLAB_ROWS else (stop - 1) // CHUNK_ROWS
+                if at == chunk:
+                    mine.append(group)
+            if mine:
+                assert mine == list(range(mine[0], mine[-1] + 1))
+                table[slab, number] = mine[0], mine[-1] + 1
+    return table.reshape(-1)
+
+
+def unpack_kernel(chunk, table_ref, core_ref, *refs):
+    last = chunk == NUM_CHUNKS - 1
+    pairs = 1 + (chunk > 0) + last
+    sources = refs[:2 * pairs]
+    outs, scratch = refs[-7 - 11:-11], refs[-11:]
+    stage, carry_in, head_in, wide, out_q, out_w, out_f, load_sem, sem_q, sem_w, sem_f = scratch
+    core = core_ref[0]
+    slots = 4
+    end_row = CARRY_ROWS + SLAB_ROWS - chunk * CHUNK_ROWS
+
+    def load(slab, slot, act):
+        def both(pair, owner, rows, target, number):
+            chip, parity = owner // 2, lax.rem(owner, 2)
+            for which in range(2):
+                @pl.when((parity == core) if which == 0 else (parity != core))
+                def _():
+                    act(pltpu.make_async_copy(sources[2 * pair + which].at[chip, rows, :], target.at[slot],
+                                              load_sem.at[slot, number]))
+        both(0, slab, pl.ds(0, CHUNK_ROWS), stage, 0)
+        if chunk > 0:
+            both(1, slab, pl.ds(CHUNK_ROWS - CARRY_ROWS, CARRY_ROWS), carry_in, 1)
+        if last:
+            @pl.when(slab < 7)
+            def _():
+                both(2, slab + 1, pl.ds(0, CARRY_ROWS), head_in, 2)
+
+    load(0, 0, lambda copy: copy.start())
+
+    def widen(source, slot, rows, target_row):
+        def body(step, carry):
+            base = pl.multiple_of(step * 32, 32)
+            wide[pl.ds(target_row + base, 32), :] = source[slot, pl.ds(base, 32), :].astype(jnp.float32)
+            return carry
+        lax.fori_loop(0, rows // 32, body, 0)
+
+    def groups(slab, number, ring, sem, fill, place):
+        low = table_ref[(slab * 7 + number) * 2]
+        high = table_ref[(slab * 7 + number) * 2 + 1]
+        name = NAMES[number]
+        origin = ROW_BASE[name] - chunk * CHUNK_ROWS + CARRY_ROWS - slab * SLAB_ROWS
+
+        def copy(group, slot):
+            return pltpu.make_async_copy(ring.at[slot], place(group), sem.at[slot])
+
+        def body(group, carry):
+            slot = lax.rem(group - low, slots)
+
+            @pl.when(group - low >= slots)
+            def _():
+                copy(group, slot).wait()
+            fill(origin + group * GROUP_ROWS[name], ring, slot)
+            copy(group, slot).start()
+            return carry
+        lax.fori_loop(low, high, body, 0)
+
+        def drain(slot, carry):
+            copy(0, slot).wait()
+            return carry
+        lax.fori_loop(0, jnp.minimum(high - low, slots), drain, 0)
+
+    def fill_rows(row, ring, slot):
+        for part in range(8):
+            ring[slot, pl.ds(part * 32, 32), :] = wide[pl.ds(row + part * 32, 32), :].astype(jnp.bfloat16)
+
+    def fill_tiles(tiles):
+        def fill(row, ring, slot):
+            for tile in range(tiles):
+                ring[slot, :, pl.ds(tile * LANES, LANES)] = wide[pl.ds(row + tile, 16, stride=tiles), :].astype(jnp.bfloat16)
+        return fill
+
+    def slab_step(slab, carry):
+        slot = lax.rem(slab, 2)
+        load(slab, slot, lambda copy: copy.wait())
+
+        @pl.when(slab < 7)
+        def _():
+            load(slab + 1, 1 - slot, lambda copy: copy.start())
+        widen(stage, slot, CHUNK_ROWS, CARRY_ROWS)
+        if chunk > 0:
+            widen(carry_in, slot, CARRY_ROWS, 0)
+        if last:
+            @pl.when(slab < 7)
+            def _():
+                widen(head_in, slot, CARRY_ROWS, end_row)
+        for number in range(3):
+            groups(slab, number, out_q, sem_q, fill_rows,
+                   lambda group, number=number: outs[number].at[pl.ds(pl.multiple_of(group * 256, 256), 256), :])
+        for number, tiles, ring, sem in ((3, 16, out_w, sem_w), (4, 43, out_f, sem_f), (5, 43, out_f, sem_f),
+                                         (6, 16, out_w, sem_w)):
+            groups(slab, number, ring, sem, fill_tiles(tiles),
+                   lambda group, number=number: outs[number].at[pl.ds(pl.multiple_of(group * 16, 16), 16), :])
+        return carry
+
+    lax.fori_loop(0, 8, slab_step, 0)
+
+
+def unpack_chunk(chunk, core_vec, arrays, done):
+    any_spec = pl.BlockSpec(memory_space=pl.ANY)
+    bf16 = jnp.bfloat16
+    shapes = [(32768, LANES)] * 3 + [(2048, 2048), (2048, 5504), (2048, 5504), (5504, 2048)]
+    return pl.pallas_call(
+        functools.partial(unpack_kernel, chunk),
+        grid_spec=pltpu.PrefetchScalarGridSpec(
+            num_scalar_prefetch=2, grid=(),
+            in_specs=[any_spec] * (len(arrays) + len(done)),
+            out_specs=(any_spec,) * 7,
+            scratch_shapes=[
+                pltpu.VMEM((2, CHUNK_ROWS, LANES), bf16),
+                pltpu.VMEM((2, CARRY_ROWS, LANES), bf16),
+                pltpu.VMEM((2, CARRY_ROWS, LANES), bf16),
+                pltpu.VMEM((CHUNK_ROWS + 2 * CARRY_ROWS, LANES), jnp.float32),
+                pltpu.VMEM((4, 256, LANES), bf16),
+                pltpu.VMEM((4, 16, 2048), bf16),
+                pltpu.VMEM((4, 16, 5504), bf16),
+                pltpu.SemaphoreType.DMA((2, 3)),
+                pltpu.SemaphoreType.DMA((4,)),
+                pltpu.SemaphoreType.DMA((4,)),
+                pltpu.SemaphoreType.DMA((4,)),
+            ]),
+        out_shape=tuple(jax.ShapeDtypeStruct(shape, bf16) for shape in shapes),
+        input_output_aliases={2 + len(arrays) + n: n for n in range(len(done))},
+        compiler_params=pltpu.CompilerParams(vmem_limit_bytes=40 * 2 ** 20),
+        cost_estimate=pl.CostEstimate(flops=10 ** 7, bytes_accessed=4 * 8 * CHUNK_ROWS * LANES, transcendentals=0),
+        name=f'unpack_{chunk}',
+    )(jnp.asarray(group_table(chunk)), core_vec, *arrays, *done)
 
 
 def solution(mesh):
-    dp_size = mesh.shape['dp']
+    same_core = [[0, 2, 4, 6], [1, 3, 5, 7]]
+    partner = [(dev, dev ^ 1) for dev in range(8)]
 
     def per_device(x_loc, dy_loc, pos_loc, attn_gain, w_query, w_key, w_value, w_out, mlp_gain, w_gate, w_up, w_down, master_loc, mean_loc, var_loc):
         w_list = (attn_gain, w_query, w_key, w_value, w_out, mlp_gain, w_gate, w_up, w_down)
-        grad_x, flat_grad = local_grads(x_loc, dy_loc, pos_loc, w_list)
-        grad_shard = lax.psum_scatter(flat_grad, 'dp', scatter_dimension=0, tiled=True).astype(jnp.float32) / dp_size
-        grad_norm = jnp.sqrt(lax.psum(jnp.sum(grad_shard * grad_shard), 'dp'))
-        shard_len = master_loc.shape[0]
-        shard_start = lax.axis_index('dp') * shard_len
-        new_master, new_mean, new_var = adamw_apply(grad_shard, grad_norm, master_loc, mean_loc, var_loc, shard_start, attn_gain.shape[0], gain_offset(w_list))
-        gathered = lax.all_gather(new_master.astype(jnp.bfloat16), 'dp', tiled=True)
-        new_weights = split_flat(gathered, w_list)
-        return (grad_x,) + tuple(new_weights) + (new_master, new_mean, new_var, grad_norm)
+        me = lax.axis_index('dp')
+        grad_x, grad_list = local_grads(x_loc, dy_loc, pos_loc, w_list)
+        shards = []
+        sum_sq = 0.0
+        for number in (1, 2, 3, 4, 6, 7, 8):
+            shard = lax.psum_scatter(grad_list[number].astype(jnp.bfloat16), 'dp', scatter_dimension=0, tiled=True)
+            sum_sq += jnp.sum(jnp.square(shard.astype(jnp.float32)))
+            shards.append(shard.reshape(-1, LANES))
+        gain_rows = jnp.concatenate([grad_list[0].astype(jnp.bfloat16).reshape(16, LANES),
+                                     grad_list[5].astype(jnp.bfloat16).reshape(16, LANES)])
+        grad_rows, all_gains, all_sums = regroup(shards, gain_rows, jnp.full((8, LANES), sum_sq / (8 * LANES)))
+        gain_sum = jnp.sum(all_gains.astype(jnp.float32), axis=0)
+        grad_norm = jnp.sqrt(jnp.sum(all_sums) + jnp.sum(gain_sum * gain_sum)) / 8.0
+        clip_scale = jnp.minimum(1.0, 1.0 / (grad_norm + 1e-6))
+        gain_low = gain_sum.astype(jnp.bfloat16)
+        gain_at = jnp.where(me == 0, 0, jnp.where(me == 2, GAIN_TWO_ROW - frame_start(2), GRAD_ROWS - 16))
+        grad_rows = lax.dynamic_update_slice(grad_rows, jnp.where(me == 0, gain_low[:16], gain_low[16:]), (gain_at, 0))
+        state = [vec.reshape(SLAB_ROWS, LANES) for vec in (master_loc, mean_loc, var_loc)]
+        me_vec = me.astype(jnp.int32)[None]
+        scale_vec = (clip_scale / 8.0)[None]
+        done = ()
+        gathered = []
+        for chunk in range(NUM_CHUNKS):
+            *done, low = adamw_chunk(chunk, me_vec, scale_vec, grad_rows, state, done)
+            own = lax.all_gather(low, 'dp', axis_index_groups=same_core)
+            gathered.append((own, lax.ppermute(own, 'dp', partner)))
+        new_state = [rows.reshape(-1) for rows in done]
+        core_vec = lax.rem(me_vec, 2)
+        weights = ()
+        for chunk in range(NUM_CHUNKS):
+            arrays = gathered[chunk] + (gathered[chunk - 1] if chunk > 0 else ()) + (gathered[0] if chunk == NUM_CHUNKS - 1 else ())
+            weights = unpack_chunk(chunk, core_vec, arrays, weights)
+        even = core_vec[0] == 0
+        gain_outs = []
+        for row in (0, GAIN_TWO_ROW):
+            slab, local = row // SLAB_ROWS, row % SLAB_ROWS
+            chunk, first = local // CHUNK_ROWS, local % CHUNK_ROWS
+            mine, other = (pair[slab // 2, first:first + 16] for pair in gathered[chunk])
+            gain_outs.append(jnp.where(even, mine, other).reshape(-1))
+        return (grad_x, gain_outs[0], weights[0].reshape(w_query.shape), weights[1].reshape(w_key.shape),
+                weights[2].reshape(w_value.shape), weights[3].reshape(w_out.shape), gain_outs[1], weights[4],
+                weights[5], weights[6], *new_state, grad_norm)
 
     in_specs = (P('dp'),) * 3 + (P(),) * 9 + (P('dp'),) * 3
     out_specs = (P('dp'),) + (P(),) * 9 + (P('dp'),) * 3 + (P(),)

time: 4810 us -> 2550 us (0.53)
  waiting for transfers between devices: 1970 us -> 761 us
  local copies, waits for them, and re-layouts: 1110 us -> 148 us
  other arithmetic: 838 us -> 234 us
  Pallas kernels: 0 us -> 530 us
    unnamed x3 -> x11, waiting for transfers between devices: 1120 us -> 0.18 us
    unnamed x96 -> x90, local copies, waits for them, and re-layouts: 735 us -> 50.9 us
    all_gather x1 -> x0, other arithmetic: 548 us -> none  [per_device(): gathered = lax.all_gather(new_master.astype(jnp.bfloat16), 'dp', tiled=True)]
    pallas_call x0 -> x9, Pallas kernels: none -> 530 us  [the longest x4 298 us: unpack_chunk(): pl.pallas_call(functools.partial(unpack_kernel, chunk), grid_spec=pltpu.P...]
    all_gather x1 -> x4, waiting for transfers between devices: 858 us -> 431 us  [per_device(): own = lax.all_gather(low, 'dp', axis_index_groups=same_core)]
    reduce_scatter x0 -> x7, waiting for transfers between devices: none -> 329 us  [per_device(): lax.psum_scatter(grad_list[number].astype(jnp.bfloat16), 'dp', scatter_di...]
    reshape x5 -> x7, local copies, waits for them, and re-layouts: 183 us -> 25.8 us  [per_device(): shards.append(shard.reshape(-1, LANES))]
    slice x4 -> x0, local copies, waits for them, and re-layouts: 102 us -> none  [split_flat(): pieces.append(flat_vec[offset:offset + weight.size].reshape(weight.shape))]
  transfers between devices with their start and end apart: 2 -> 15, of which waited for: 2 -> 7; matrix products, arithmetic and copies ran while one was open for 0% -> 14% of each run, Pallas kernels for 0% -> 11%
where the time goes in v1:
time: 2550 us; the launch traced here: 2540 us
  matrix products  842 us (33%)
  waiting for transfers between devices  761 us (30%)
  Pallas kernels  530 us (21%)
  other arithmetic  234 us (9%)
  local copies, waits for them, and re-layouts  148 us (6%)
    all_gather x4, waiting for transfers between devices, per_device(): own = lax.all_gather(low, 'dp', axis_index_groups=same_core)  431 us
    reduce_scatter x7, waiting for transfers between devices, per_device(): lax.psum_scatter(grad_list[number].astype(jnp.bfloat16), 'dp', scatter_di...  329 us
    pallas_call x4, Pallas kernels, unpack_chunk(): pl.pallas_call(functools.partial(unpack_kernel, chunk), grid_spec=pltpu.P...  298 us
    pallas_call x1, Pallas kernels, regroup(): pl.pallas_call(regroup_kernel, out_shape=(jax.ShapeDtypeStruct((GRAD_ROWS...  146 us
    pallas_call x4, Pallas kernels, adamw_chunk(): pl.pallas_call(functools.partial(adamw_kernel, chunk), grid_spec=pltpu.Pr...  85.9 us
    dot_general x1, matrix products, local_grads(): jnp.einsum('nd,fd->nf', dy_flat, w_down, preferred_element_type=jnp.float32)  64.2 us
    another operation x1, other arithmetic  60.1 us
    dot_general x1, matrix products, local_grads(): jnp.einsum('bqkgd,bskd->bkgqs', d_context, v_heads, preferred_element_typ...  56.1 us
  transfers between devices with their start and end apart: 15, of which 7 were waited for; matrix products, arithmetic and copies ran while one was open for 14% of the time, Pallas kernels for 11%

profile of v1, /device:TPU:0, one launch (start us, length us, event | category | flops | bytes accessed | tf_op | source)
XLA Modules:
  0.0 2536.0 jit_solution(2587991332844969619)
XLA Ops:
  144.3 23.6 fusion.28
  167.9 31.3 %fusion.6 = (f32[2,16,768]{2,1,0:T(8,128)S(1)}, f32[2,16,768,768]{3,2,1,0:T(8,128)}) fusion(pred[768,768]{0,1:T(8,128)(4,1)S(1)} %iota_compare_fusion, bf16[2,768,16,128]{1,3,2,0:T(8,128)(2,1)} %get-tuple-element.123, bf16[2,768,16,128]{1,3,2,0:T(8,128)(2,1)} %get-tuple-element.122), kind=kOutput, calls=%fused_computation.10 | convolution fusion | flops 4888436736 | bytes 88768512 | tf_op jit(solution)/shard_map/bqkgd,bskd->bkgqs/dot_general | solution.py:75
  199.2 24.1 fusion.5
  223.3 32.5 %convert_bitcast_fusion.1 = bf16[2,768,16,1,128]{1,4,2,0,3:T(8,128)(2,1)} fusion(bf16[2,768,16,128]{3,2,1,0:T(8,128)(2,1)} %bitcast.290, f32[2,16,768]{2,1,0:T(8,128)S(1)} %fusion.5, f32[2,16,768]{2,1,0:T(8,128)S(1)} %get-tuple-element.132, f32[2,16,768,768]{3,2,1,0:T(8,128)} %get-tuple-element.133, pred[768,768]{0,1:T(8,128)(4,1)S(1)} %iota_compare_fusion), kind=kOutput, calls=%fused_computation.107 | convolution fusion | flops 4929355776 | bytes 88866816 | tf_op jit(solution)/shard_map/bkgqs,bskd->bqkgd/dot_general | solution.py:79
  286.4 45.8 %fusion.104 = f32[1536,5504]{1,0:T(8,128)} fusion(bf16[2048,5504]{1,0:T(8,128)(2,1)} %param.28, bf16[1536,2048]{1,0:T(8,128)(2,1)} %get-tuple-element.135, f32[2048]{0:T(1024)S(1)} %convert_element_type.193, f32[1536]{0:T(1024)S(1)} %add_rsqrt_fusion), kind=kOutput, calls=%fused_computation.152 | convolution fusion | flops 34640756736 | bytes 62666752 | tf_op jit(solution)/shard_map/dot_general | solution.py:86
  332.2 45.9 %fusion.106 = f32[1536,5504]{1,0:T(8,128)} fusion(bf16[2048,5504]{1,0:T(8,128)(2,1)} %param.29, bf16[1536,2048]{1,0:T(8,128)(2,1)} %get-tuple-element.135, f32[2048]{0:T(1024)S(1)} %convert_element_type.193, f32[1536]{0:T(1024)S(1)} %add_rsqrt_fusion), kind=kOutput, calls=%fused_computation.153 | convolution fusion | flops 34640756736 | bytes 62666752 | tf_op jit(solution)/shard_map/dot_general | solution.py:87
  378.1 64.2 %multiply_convert_fusion.1 = (bf16[1536,5504]{1,0:T(8,128)(2,1)}, bf16[1536,5504]{1,0:T(8,128)(2,1)}) fusion(f32[1536,5504]{1,0:T(8,128)} %fusion.104, f32[1536,5504]{1,0:T(8,128)} %fusion.106, bf16[1536,2048]{1,0:T(8,128)(2,1)} %bitcast.277, bf16[5504,2048]{1,0:T(8,128)(2,1)} %param.30), kind=kOutput, calls=%fused_computation.17 | convolution fusion | flops 34738077696 | bytes 130285568 | tf_op jit(solution)/shard_map/nd,fd->nf/dot_general | solution.py:92
  442.3 46.2 %fusion.111 = f32[1536,2048]{1,0:T(8,128)} fusion(bf16[1536,5504]{1,0:T(8,128)(2,1)} %get-tuple-element.113, bf16[2048,5504]{1,0:T(8,128)(2,1)} %param.28), kind=kOutput, calls=%fused_computation.157 | convolution fusion | flops 34628173824 | bytes 52035584 | tf_op jit(solution)/shard_map/nf,df->nd/dot_general | solution.py:97
  488.5 50.9 %fusion.23 = (bf16[2048]{0:T(1024)(128)(2,1)}, f32[1536]{0:T(1024)S(1)}, f32[1536,2048]{1,0:T(8,128)}) fusion(bf16[1536,2048]{1,0:T(8,128)(2,1)} %get-tuple-element.135, f32[1536]{0:T(1024)S(1)} %copy-done.32, f32[2048]{0:T(1024)S(1)} %copy-done.35, f32[1536,2048]{1,0:T(8,128)} %fusion.111, bf16[1536,5504]{1,0:T(8,128)(2,1)} %get-tuple-element.112, ...), kind=kOutput, calls=%fused_computation.36 | convolution fusion | flops 34653339648 | bytes 70934528 | tf_op jit(solution)/shard_map/nf,df->nd/dot_general | solution.py:98
  587.0 56.1 %fusion = (f32[2,16,768]{2,1,0:T(8,128)S(1)}, f32[2,16,768,768]{3,2,1,0:T(8,128)}) fusion(f32[2,16,768]{2,1,0:T(8,128)S(1)} %copy-done.22, f32[2,16,768]{2,1,0:T(8,128)S(1)} %copy-done.19, f32[2,16,768,768]{3,2,1,0:T(8,128)} %get-tuple-element.133, pred[768,768]{0,1:T(8,128)(4,1)S(1)} %copy-done.10, bf16[2,768,16,128]{1,3,2,0:T(8,128)(2,1)} %copy.88, ...), kind=kOutput, calls=%fused_computation.3 | convolution fusion | flops 4945059840 | bytes 164462592 | tf_op jit(solution)/shard_map/bqkgd,bskd->bkgqs/dot_general | solution.py:105
  643.1 60.1 %fusion.7 = bf16[2,16,768,768]{2,3,1,0:T(8,128)(2,1)} fusion(f32[2,16,768,768]{3,2,1,0:T(8,128)} %get-tuple-element.138, f32[2,16,768]{2,1,0:T(8,128)S(1)} %get-tuple-element.137, f32[2,16,768]{2,1,0:T(8,128)S(1)} %copy-done.22, f32[2,16,768]{2,1,0:T(8,128)S(1)} %copy-done.19, f32[2,16,768,768]{3,2,1,0:T(8,128)} %get-tuple-element.133, ...), kind=kLoop, calls=%fused_computation.11 | loop fusion | flops 150994944 | bytes 189628416 | tf_op jit(solution)/shard_map/reshape.9
  724.5 31.4 %bitcast_multiply_fusion.1 = (f32[2,768,16,128]{1,3,2,0:T(8,128)}, f32[2,768,16,128]{1,3,2,0:T(8,128)}, f32[2,16,128,768]{3,2,1,0:T(8,128)}) fusion(f32[2,768,128]{1,2,0:T(8,128)S(1)} %copy-done.13, f32[2,16,128,768]{3,2,1,0:T(8,128)} %fusion.112, bf16[2,768,16,128]{1,3,2,0:T(8,128)(2,1)} %get-tuple-element.122, bf16[2,16,768,768]{2,3,1,0:T(8,128)(2,1)} %fusion.7), kind=kOutput, calls=%fused_computation.48 | convolution fusion | flops 4838129664 | bytes 95158272 | tf_op jit(solution)/shard_map/bkgqs,bqkgd->bskd/dot_general | solution.py:109
  777.9 23.1 fusion.30
  858.5 33.2 %convert_bitcast_fusion = bf16[2,768,16,128]{1,3,2,0:T(8,128)(2,1)} fusion(bf16[2,768,16,128]{1,3,2,0:T(8,128)(2,1)} %copy.88, f32[2,16,768]{2,1,0:T(8,128)S(1)} %copy-done.23, f32[2,16,768]{2,1,0:T(8,128)S(1)} %copy-done.20, f32[2,16,768,768]{3,2,1,0:T(8,128)} %get-tuple-element.133, pred[768,768]{0,1:T(8,128)(4,1)S(1)} %copy-done.11), kind=kOutput, calls=%fused_computation.106 | convolution fusion | flops 4929355776 | bytes 88866816 | tf_op jit(solution)/shard_map/bkgqs,bqkgd->bskd/dot_general | solution.py:106
  941.3 46.0 %convolution_convert_fusion.2 = bf16[2048,5504]{1,0:T(8,128)(2,1)} fusion(bf16[1536,5504]{1,0:T(8,128)(2,1)} %get-tuple-element.113, bf16[1536,2048]{1,0:T(8,128)(2,1)} %get-tuple-element.135, f32[2048]{0:T(1024)S(1)} %copy-done.36, f32[1536]{0:T(1024)S(1)} %copy-done.33), kind=kOutput, calls=%fused_computation.24 | convolution fusion | flops 34652028928 | bytes 45758464 | tf_op jit(solution)/shard_map/nd,nf->df/dot_general | solution.py:95
  987.4 46.4 %convolution_convert_fusion.1 = bf16[2048,5504]{1,0:T(8,128)(2,1)} fusion(bf16[1536,5504]{1,0:T(8,128)(2,1)} %get-tuple-element.112, bf16[1536,2048]{1,0:T(8,128)(2,1)} %get-tuple-element.135, f32[2048]{0:T(1024)S(1)} %copy-done.36, f32[1536]{0:T(1024)S(1)} %copy-done.33), kind=kOutput, calls=%fused_computation.23 | convolution fusion | flops 34652028928 | bytes 45758464 | tf_op jit(solution)/shard_map/nd,nf->df/dot_general | solution.py:96
  1033.9 48.3 %convolution_convert_fusion = bf16[5504,2048]{1,0:T(8,128)(2,1)} fusion(bf16[1536,2048]{1,0:T(8,128)(2,1)} %bitcast.278, f32[1536,5504]{1,0:T(8,128)} %fusion.106, f32[1536,5504]{1,0:T(8,128)} %fusion.104), kind=kOutput, calls=%fused_computation.22 | convolution fusion | flops 34690170880 | bytes 96468992 | tf_op jit(solution)/shard_map/nf,nd->fd/dot_general | solution.py:91
  1119.9 27.3 %fusion.39 = (bf16[2048]{0:T(1024)(128)(2,1)S(1)}, f32[1536]{0:T(1024)}, f32[1536,2048]{1,0:T(8,128)}) fusion(bf16[2,768,2048]{2,1,0:T(8,128)(2,1)} %param.19, f32[1536]{0:T(1024)S(1)} %rsqrt.21, f32[2048]{0:T(1024)S(1)} %copy-done.25, bf16[256,8,16,128]{3,2,1,0:T(8,128)(2,1)} %bitcast.301, bf16[192,8,16,128]{3,2,1,0:T(8,128)(2,1)} %bitcast.289, ...), kind=kOutput, calls=%fused_computation.64 | convolution fusion | flops 12913209344 | bytes 58744832 | tf_op jit(solution)/shard_map/nc,dc->nd/dot_general | solution.py:118
  1169.3 62.1 %reduce-scatter.16.cloned.1.call-done = bf16[256,5504]{1,0:T(8,128)(2,1)} async-done(((bf16[2048,5504]{1,0:T(8,128)(2,1)}), bf16[256,5504]{1,0:T(8,128)(2,1)}) %reduce-scatter.16.cloned.1.call-update) | async-done | bytes 2818064 | tf_op jit(solution)/shard_map/reduce_scatter | solution.py:457
  1235.9 133.5 %reduce-scatter.18.cloned.1.call-done = bf16[256,5504]{1,0:T(8,128)(2,1)} async-done(((bf16[2048,5504]{1,0:T(8,128)(2,1)}), bf16[256,5504]{1,0:T(8,128)(2,1)}) %reduce-scatter.18.cloned.1.call-update) | async-done | bytes 2818064 | tf_op jit(solution)/shard_map/reduce_scatter | solution.py:457
  1374.0 133.5 %reduce-scatter.20.cloned.1.call-done = bf16[688,2048]{1,0:T(8,128)(2,1)} async-done(((bf16[5504,2048]{1,0:T(8,128)(2,1)}), bf16[688,2048]{1,0:T(8,128)(2,1)}) %reduce-scatter.20.cloned.1.call-update) | async-done | bytes 2818064 | tf_op jit(solution)/shard_map/reduce_scatter | solution.py:457
  1529.1 146.5 %regroup.1 = (bf16[49552,128]{1,0:T(8,128)(2,1)}, bf16[8,32,128]{2,1,0:T(8,128)(2,1)}, f32[8,8,128]{2,1,0:T(8,128)}) custom-call(bf16[4096,128]{1,0:T(8,128)(2,1)} %reshape.328.refs_0_, bf16[4096,128]{1,0:T(8,128)(2,1)} %reshape.329.refs_1_, bf16[4096,128]{1,0:T(8,128)(2,1)} %reshape.330.refs_2_, bf16[4096,128]{1,0:T(8,128)(2,1)} %reshape.331.refs_3_, ...), custom_call_target="tpu_custom_call" | custom-call | tf_op jit(solution)/shard_map/regroup/pallas_call | solution.py:221
  1680.4 21.5 adamw_0.1
  1702.1 21.5 adamw_1.1
  1766.6 71.5 %all-gather.9.cloned.1.call-done = bf16[49536,128]{1,0:T(8,128)(2,1)} async-done(((bf16[12384,128]{1,0:T(8,128)(2,1)}), bf16[49536,128]{1,0:T(8,128)(2,1)}) %all-gather.9.cloned.1.call-update) | async-done | bytes 12681232 | tf_op jit(solution)/shard_map/all_gather | solution.py:476
  1838.2 120.0 %all-gather.15.cloned.1.call-done = bf16[49536,128]{1,0:T(8,128)(2,1)} async-done(((bf16[12384,128]{1,0:T(8,128)(2,1)}), bf16[49536,128]{1,0:T(8,128)(2,1)}) %all-gather.15.cloned.1.call-update) | async-done | bytes 12681232 | tf_op jit(solution)/shard_map/all_gather | solution.py:476
  1958.2 119.9 %all-gather.13.cloned.1.call-done = bf16[49536,128]{1,0:T(8,128)(2,1)} async-done(((bf16[12384,128]{1,0:T(8,128)(2,1)}), bf16[49536,128]{1,0:T(8,128)(2,1)}) %all-gather.13.cloned.1.call-update) | async-done | bytes 12681232 | tf_op jit(solution)/shard_map/all_gather | solution.py:476
  2078.1 120.0 %all-gather.11.cloned.1.call-done = bf16[49536,128]{1,0:T(8,128)(2,1)} async-done(((bf16[12384,128]{1,0:T(8,128)(2,1)}), bf16[49536,128]{1,0:T(8,128)(2,1)}) %all-gather.11.cloned.1.call-update) | async-done | bytes 12681232 | tf_op jit(solution)/shard_map/all_gather | solution.py:476
  2214.1 70.0 %unpack_0.1 = (bf16[32768,128]{1,0:T(8,128)(2,1)}, bf16[32768,128]{1,0:T(8,128)(2,1)}, bf16[32768,128]{1,0:T(8,128)(2,1)}, bf16[2048,2048]{1,0:T(8,128)(2,1)}, b...) custom-call(s32[112]{0:T(128)S(1)} %copy-done.4, s32[1]{0:T(128)S(6)} %rem.18.core_ref, ...), custom_call_target="tpu_custom_call" | custom-call | flops 10000000 | bytes 50724864 | tf_op jit(solution)/shard_map/unpack_0/pallas_call | solution.py:419
  2288.7 77.0 %unpack_1.1 = (bf16[32768,128]{1,0:T(8,128)(2,1)}, bf16[32768,128]{1,0:T(8,128)(2,1)}, bf16[32768,128]{1,0:T(8,128)(2,1)}, bf16[2048,2048]{1,0:T(8,128)(2,1)}, b...) custom-call(s32[112]{0:T(128)S(1)} %copy-done.7, ...), custom_call_target="tpu_custom_call", output_to_operand_aliasing={{0}: (6, {}), {1}: (7, {}), {2}: (8, {}), {3}: (9, {}), {4}... | custom-call | flops 10000000 | bytes 50724864 | tf_op jit(solution)/shard_map/unpack_1/pallas_call | solution.py:419
  2370.3 77.2 %unpack_2.1 = (bf16[32768,128]{1,0:T(8,128)(2,1)}, bf16[32768,128]{1,0:T(8,128)(2,1)}, bf16[32768,128]{1,0:T(8,128)(2,1)}, bf16[2048,2048]{1,0:T(8,128)(2,1)}, b...) custom-call(s32[112]{0:T(128)S(1)} %copy-done.6, ...), custom_call_target="tpu_custom_call", output_to_operand_aliasing={{0}: (6, {}), {1}: (7, {}), {2}: (8, {}), {3}: (9, {}), {4}... | custom-call | flops 10000000 | bytes 50724864 | tf_op jit(solution)/shard_map/unpack_2/pallas_call | solution.py:419
  2454.7 73.4 %unpack_3.1 = (bf16[32768,128]{1,0:T(8,128)(2,1)}, bf16[32768,128]{1,0:T(8,128)(2,1)}, bf16[32768,128]{1,0:T(8,128)(2,1)}, bf16[2048,2048]{1,0:T(8,128)(2,1)}, b...) custom-call(s32[112]{0:T(128)S(1)} %copy-done.5, ...), custom_call_target="tpu_custom_call", output_to_operand_aliasing={{0}: (8, {}), {1}: (9, {}), {2}: (10, {}), {3}: (11, {}), {... | custom-call | flops 10000000 | bytes 50724864 | tf_op jit(solution)/shard_map/unpack_3/pallas_call | solution.py:419
  (187 shorter events, 530.0 us)
Async XLA Ops:
  7.2 1140.7 %reduce-scatter.8.cloned.1.call-start = ((), (), s32[]{:S(2)}) async-start(), calls=%async_computation.7 | async-start | bytes 9437184 | tf_op jit(solution)/shard_map/reduce_scatter | solution.py:457
  7.4 215.9 %copy-start.9 = (pred[768,768]{0,1:T(8,128)(4,1)}, pred[768,768]{0,1:T(8,128)(4,1)S(1)}, u32[]{:S(2)}) copy-start(pred[768,768]{0,1:T(8,128)(4,1)S(1)} %iota_compare_fusion) | copy-start | bytes 1769476
  8.2 27.1 %copy-start.24 = (f32[2048]{0:T(1024)}, f32[2048]{0:T(1024)S(1)}, u32[]{:S(2)}) copy-start(f32[2048]{0:T(1024)S(1)} %convert_element_type.178) | copy-start | bytes 24580
  199.2 24.1 copy-start.18
  223.3 32.6 %copy-start.21 = (f32[2,16,768]{2,1,0:T(8,128)}, f32[2,16,768]{2,1,0:T(8,128)S(1)}, u32[]{:S(2)}) copy-start(f32[2,16,768]{2,1,0:T(8,128)S(1)} %fusion.5) | copy-start | bytes 294916
  286.3 45.9 %copy-start.31 = (f32[1536]{0:T(1024)}, f32[1536]{0:T(1024)S(1)}, u32[]{:S(2)}) copy-start(f32[1536]{0:T(1024)S(1)} %add_rsqrt_fusion) | copy-start | bytes 18436
  286.4 45.8 %copy-start.34 = (f32[2048]{0:T(1024)}, f32[2048]{0:T(1024)S(1)}, u32[]{:S(2)}) copy-start(f32[2048]{0:T(1024)S(1)} %convert_element_type.193) | copy-start | bytes 24580
  442.3 46.2 %copy-start.32 = (f32[1536]{0:T(1024)S(1)}, f32[1536]{0:T(1024)}, u32[]{:S(2)}) copy-start(f32[1536]{0:T(1024)} %copy-done.31) | copy-start | bytes 18436
  442.3 46.2 %copy-start.35 = (f32[2048]{0:T(1024)S(1)}, f32[2048]{0:T(1024)}, u32[]{:S(2)}) copy-start(f32[2048]{0:T(1024)} %copy-done.34) | copy-start | bytes 24580
  829.5 320.7 %reduce-scatter.10.cloned.1.call-start = ((), (), s32[]{:S(2)}) async-start(), calls=%async_computation.8 | async-start | bytes 9437184 | tf_op jit(solution)/shard_map/reduce_scatter | solution.py:457
  858.5 295.4 %reduce-scatter.12.cloned.1.call-start = ((), (), s32[]{:S(2)}) async-start(), calls=%async_computation.9 | async-start | bytes 9437184 | tf_op jit(solution)/shard_map/reduce_scatter | solution.py:457
  920.0 236.9 %reduce-scatter.14.cloned.1.call-start = ((), (), s32[]{:S(2)}) async-start(), calls=%async_computation.10 | async-start | bytes 9437184 | tf_op jit(solution)/shard_map/reduce_scatter | solution.py:457
  941.3 290.1 %reduce-scatter.16.cloned.1.call-start = ((), (), s32[]{:S(2)}) async-start(), calls=%async_computation.11 | async-start | bytes 25362432 | tf_op jit(solution)/shard_map/reduce_scatter | solution.py:457
  987.4 382.0 %reduce-scatter.18.cloned.1.call-start = ((), (), s32[]{:S(2)}) async-start(), calls=%async_computation.12 | async-start | bytes 25362432 | tf_op jit(solution)/shard_map/reduce_scatter | solution.py:457
  1033.9 473.7 %reduce-scatter.20.cloned.1.call-start = ((), (), s32[]{:S(2)}) async-start(), calls=%async_computation.13 | async-start | bytes 25362432 | tf_op jit(solution)/shard_map/reduce_scatter | solution.py:457
  1082.2 755.9 %all-gather.9.cloned.1.call-start = ((), (), s32[]{:S(2)}) async-start(), calls=%async_computation.14 | async-start | bytes 15851520 | tf_op jit(solution)/shard_map/all_gather | solution.py:476
  1082.9 37.0 %copy-start.29 = (f32[1536]{0:T(1024)}, f32[1536]{0:T(1024)S(1)}, u32[]{:S(2)}) copy-start(f32[1536]{0:T(1024)S(1)} %rsqrt.21) | copy-start | bytes 18436
  1119.9 27.3 %copy-start.40 = (bf16[2048]{0:T(1024)(128)(2,1)S(1)}, bf16[2048]{0:T(1024)(128)(2,1)}, u32[]{:S(2)}) copy-start(bf16[2048]{0:T(1024)(128)(2,1)} %get-tuple-element.110) | copy-start | bytes 12292
  1369.4 149.2 %copy-start.14 = (bf16[256,5504]{1,0:T(8,128)(2,1)S(1)}, bf16[256,5504]{1,0:T(8,128)(2,1)}, u32[]{:S(2)}) copy-start(bf16[256,5504]{1,0:T(8,128)(2,1)} %reduce-scatter.18.cloned.1.call-done) | copy-start | bytes 8454148
  1702.0 256.2 %all-gather.15.cloned.1.call-start = ((), (), s32[]{:S(2)}) async-start(), calls=%async_computation.17 | async-start | bytes 15851520 | tf_op jit(solution)/shard_map/all_gather | solution.py:476
  1723.6 354.5 %all-gather.13.cloned.1.call-start = ((), (), s32[]{:S(2)}) async-start(), calls=%async_computation.16 | async-start | bytes 15851520 | tf_op jit(solution)/shard_map/all_gather | solution.py:476
  1745.2 452.9 %all-gather.11.cloned.1.call-start = ((), (), s32[]{:S(2)}) async-start(), calls=%async_computation.15 | async-start | bytes 15851520 | tf_op jit(solution)/shard_map/all_gather | solution.py:476
  1745.2 452.9 %copy-start.37 = (f32[1536]{0:T(1024)S(1)}, f32[1536]{0:T(1024)}, u32[]{:S(2)}) copy-start(f32[1536]{0:T(1024)} %get-tuple-element.109) | copy-start | bytes 18436
  1745.2 452.9 %copy-start.26 = (f32[2048]{0:T(1024)S(1)}, f32[2048]{0:T(1024)}, u32[]{:S(2)}) copy-start(f32[2048]{0:T(1024)} %copy-done.24) | copy-start | bytes 24580
  1745.2 452.9 %copy-start.30 = (f32[1536]{0:T(1024)S(1)}, f32[1536]{0:T(1024)}, u32[]{:S(2)}) copy-start(f32[1536]{0:T(1024)} %copy-done.29) | copy-start | bytes 18436
  1838.2 374.6 %collective-permute-start = (bf16[4,12384,128]{2,1,0:T(8,128)(2,1)}, bf16[4,12384,128]{2,1,0:T(8,128)(2,1)}, u32[]{:S(2)}, u32[]{:S(2)}) collective-permute-start(bf16[4,12384,128]{2,1,0:T(8,128)(2,1)} %bitcast.235), channel_id=1, source_target_pairs={{0,1},{1,0},{2,3},{3,2},{4,5},{5,4},{6,7},{7,6}} | collective-permute-start | bytes 38043656 | tf_op jit(solution)/shard_map/ppermute | solution.py:477
  1958.2 325.8 %collective-permute-start.3 = (bf16[4,12384,128]{2,1,0:T(8,128)(2,1)}, bf16[4,12384,128]{2,1,0:T(8,128)(2,1)}, u32[]{:S(2)}, u32[]{:S(2)}) collective-permute-start(bf16[4,12384,128]{2,1,0:T(8,128)(2,1)} %bitcast.244), channel_id=1, source_target_pairs={{0,1},{1,0},{2,3},{3,2},{4,5},{5,4},{6,7},{7,6}} | collective-permute-start | bytes 38043656 | tf_op jit(solution)/shard_map/ppermute | solution.py:477
  2078.1 287.6 %collective-permute-start.2 = (bf16[4,12384,128]{2,1,0:T(8,128)(2,1)}, bf16[4,12384,128]{2,1,0:T(8,128)(2,1)}, u32[]{:S(2)}, u32[]{:S(2)}) collective-permute-start(bf16[4,12384,128]{2,1,0:T(8,128)(2,1)} %bitcast.240), channel_id=1, source_target_pairs={{0,1},{1,0},{2,3},{3,2},{4,5},{5,4},{6,7},{7,6}} | collective-permute-start | bytes 38043656 | tf_op jit(solution)/shard_map/ppermute | solution.py:477
  2198.1 252.0 %collective-permute-start.1 = (bf16[4,12384,128]{2,1,0:T(8,128)(2,1)}, bf16[4,12384,128]{2,1,0:T(8,128)(2,1)}, u32[]{:S(2)}, u32[]{:S(2)}) collective-permute-start(bf16[4,12384,128]{2,1,0:T(8,128)(2,1)} %bitcast.247), channel_id=1, source_target_pairs={{0,1},{1,0},{2,3},{3,2},{4,5},{5,4},{6,7},{7,6}} | collective-permute-start | bytes 38043656 | tf_op jit(solution)/shard_map/ppermute | solution.py:477
  2212.8 71.3 %copy-start.7 = (s32[112]{0:T(128)S(1)}, s32[112]{0:T(128)}, u32[]{:S(2)}) copy-start(s32[112]{0:T(128)} %constant.67.clone.table_ref) | copy-start | bytes 1348
  2288.7 77.0 %copy-start.6 = (s32[112]{0:T(128)S(1)}, s32[112]{0:T(128)}, u32[]{:S(2)}) copy-start(s32[112]{0:T(128)} %constant.68.clone.table_ref) | copy-start | bytes 1348
  2370.3 79.8 %copy-start.5 = (s32[112]{0:T(128)S(1)}, s32[112]{0:T(128)}, u32[]{:S(2)}) copy-start(s32[112]{0:T(128)} %constant.69.clone.table_ref) | copy-start | bytes 1348
  (26 other events, 429.6 us)
Sparse Core Ops, SparseCore 0:
  829.6 65.0 reduce-scatter.7
  898.7 62.2 reduce-scatter.9
  965.0 62.2 reduce-scatter.11
  1031.1 62.2 reduce-scatter.13
  1097.4 133.8 reduce-scatter.15
  1235.5 133.8 reduce-scatter.17
  1373.6 133.8 reduce-scatter.19
  1702.1 135.9 all-gather.8
  1840.5 117.6 all-gather.14
  1960.4 117.6 all-gather.12
  2080.4 117.6 all-gather.10
